TPU v7x, 32 devices: a whole 2x2x4 slice. The times are simulated.
32 devices in a mesh: dp: 4 (over y, x), vocab: 8 (over z, core).
Axes of the slice: x: 2, y: 2, z: 4, core: 2. Of those that a mesh axis runs over, the one named last changes fastest.
Arguments:
- logits: bfloat16 [32, 8, 152064], P('dp', None, 'vocab'), may hold values from -40 to 250
- draft_probs: bfloat16 [32, 8, 152064], P('dp', None, 'vocab'), may hold values from 5.9185606e-07 to 1, as said below
- draft_tokens: int32 [32, 8], P('dp'), may hold values from 0 to 152063
- draft_lengths: int32 [32], P('dp'), may hold values from 1 to 8
- owner_group: int32 [32], P('dp'), may hold values from 0 to 3, as said below
Outputs:
- correction: bfloat16 [64, 152064], P('dp', 'vocab')
- accept_ratio: float32 [64, 8], P('dp')
- expected_accepted: float32 [64], P('dp')
Inputs may be any that keep to these rules, and one draw needn't show every extreme that they name: Each row of draft_probs is a distribution over the whole vocabulary whose entries are all positive. `owner_group`: no group hands more than 4 sequences to one group; some group receives exactly 4 sequences from every group.
All inputs are finite; a program needn't handle non-finite values.
Results may differ from a plain program's by a relative error of at most 0.001.
Values may be sent and summed in bfloat16 or wider, within the bound.
A program may use at most 64 MiB of HBM per device.

v0:
```python
import functools

import jax
import jax.numpy as jnp
from jax import lax
from jax.experimental import pallas as pl
from jax.experimental.pallas import tpu as pltpu
from jax.sharding import PartitionSpec as P

mixing = 0.1
LANES = 128
GROUP = 40
MIX_GROUP = 8
CHUNKS = 5
LOW = -1e30
MESH = pl.DeviceIdType.MESH


def sweep(start, stop, fn, carry, most=GROUP):
    extent = stop - start
    size = max(1, min(most, extent))
    size = min(range(max(1, size // 2), size + 1), key=lambda g: (extent % g, -g))
    whole = extent // size

    def step(i, c):
        return fn(start + i * size, size, c)

    if whole:
        carry = lax.fori_loop(0, whole, step, carry)
    rest = extent % size
    if rest:
        carry = fn(start + whole * size, rest, carry)
    return carry


def lane_tile(i):
    return pl.ds(pl.multiple_of(i * LANES, LANES), LANES)


def kernel(
    dims,
    tok_hbm, lens_hbm, own_hbm, x_hbm, d_hbm,
    out, accept_out, expected_out,
    tok, lens, own, x, d, e, send, landed, block, stat_in, spread_in, small, small_in,
    scalar_sem, load_sem, stat_ssem, stat_rsem, spr_ssem, spr_rsem, out_ssem, out_rsem, sm_ssem, sm_rsem, local_sem, store_sem,
):
    groups, vocab, capacity = dims
    seqs, depth, width = x_hbm.shape
    full = width // LANES
    tail = width - full * LANES
    tiles = e.shape[0]
    my_dp = lax.axis_index("dp")
    my_v = lax.axis_index("vocab")

    loads = []
    for n in range(seqs):
        loads.append(pltpu.make_async_copy(x_hbm.at[n], x.at[n], load_sem.at[n]))
    for n in range(seqs):
        loads.append(pltpu.make_async_copy(d_hbm.at[n], d.at[n], load_sem.at[seqs + n]))
    for n in range(seqs):
        loads[n].start()
    scalars = []
    for i, (source, target) in enumerate(((tok_hbm, tok), (lens_hbm, lens), (own_hbm, own))):
        scalars.append(pltpu.make_async_copy(source, target, scalar_sem.at[i]))
        scalars[-1].start()

    barrier = pltpu.get_barrier_semaphore()
    v_peers = [lax.rem(my_v + k, vocab) for k in range(1, vocab)]
    g_peers = [lax.rem(my_dp + k, groups) for k in range(1, groups)]
    for p in v_peers:
        pl.semaphore_signal(barrier, inc=1, device_id=(my_dp, p), device_id_type=MESH)
    for p in g_peers:
        pl.semaphore_signal(barrier, inc=1, device_id=(p, my_v), device_id_type=MESH)

    sub = lax.broadcasted_iota(jnp.int32, (depth, LANES), 0)
    lane = lax.broadcasted_iota(jnp.int32, (depth, LANES), 1)
    zero = jnp.zeros((depth, LANES), jnp.float32)

    def tail_tile(ref, n, fill):
        part = ref[n, :, pl.ds(full * LANES, tail)].astype(jnp.float32)
        return jnp.concatenate([part, jnp.full((depth, LANES - tail), fill, jnp.float32)], axis=1)

    tops = zero
    sums = zero
    for n in range(seqs):
        loads[n].wait()
        loads[seqs + n].start()

        def peak(base, count, c, n=n):
            c = list(c)
            for k in range(count):
                c[k % 4] = jnp.maximum(c[k % 4], x[n, :, lane_tile(base + k)].astype(jnp.float32))
            return tuple(c)

        first = tail_tile(x, n, LOW) if tail else jnp.full((depth, LANES), LOW, jnp.float32)
        c = sweep(0, full, peak, (first,) * 4)
        top = jnp.maximum(jnp.maximum(c[0], c[1]), jnp.maximum(c[2], c[3]))
        top = jnp.broadcast_to(jnp.max(top, axis=1, keepdims=True), (depth, LANES))

        def expo(base, count, c, n=n, top=top):
            c = list(c)
            for k in range(count):
                raw = x[n, :, lane_tile(base + k)].astype(jnp.float32)
                value = jnp.exp(raw - top)
                e[base + k, pl.ds(n * depth, depth), :] = value
                c[k % 4] = c[k % 4] + value
            return tuple(c)

        first = zero
        if tail:
            raw = tail_tile(x, n, LOW)
            first = jnp.exp(raw - top)
            e[full, pl.ds(n * depth, depth), :] = first
        c = sweep(0, full, expo, (first, zero, zero, zero))
        total = jnp.sum((c[0] + c[1]) + (c[2] + c[3]), axis=1, keepdims=True)
        tops = jnp.where(lane == n, top, tops)
        sums = jnp.where(lane == n, total, sums)
        sums = jnp.where(lane == seqs + n, top, sums)

    pl.semaphore_wait(barrier, vocab - 1 + groups - 1)

    def exchange(buf, ssem, rsem):
        copies = []
        for k in range(1, vocab):
            to = lax.rem(my_v + k, vocab)
            copies.append(pltpu.make_async_remote_copy(
                src_ref=buf.at[my_v], dst_ref=buf.at[my_v],
                send_sem=ssem.at[k], recv_sem=rsem.at[my_v],
                device_id=(my_dp, to), device_id_type=MESH,
            ))
            copies[-1].start()
        return copies

    def arrive(buf, ssem, rsem):
        for k in range(1, vocab):
            source = lax.rem(my_v + k, vocab)
            pltpu.make_async_remote_copy(
                src_ref=buf.at[source], dst_ref=buf.at[source],
                send_sem=ssem.at[k], recv_sem=rsem.at[source],
                device_id=(my_dp, source), device_id_type=MESH,
            ).wait_recv()

    stat_in[my_v] = sums
    stat_copies = exchange(stat_in, stat_ssem, stat_rsem)

    for copy in scalars:
        copy.wait()

    lens_row = jnp.zeros((depth, LANES), jnp.int32)
    slots = []
    for n in range(seqs):
        lens_row = jnp.where(lane == n, lens[n], lens_row)
        rank = jnp.int32(0)
        for i in range(n):
            rank = rank + jnp.where(own[i] == own[n], 1, 0)
        slots.append(own[n] * capacity + rank)
    live = sub < lens_row
    rows = groups * capacity
    pick_row = lax.broadcasted_iota(jnp.int32, (rows, seqs), 0)
    pick_col = lax.broadcasted_iota(jnp.int32, (rows, seqs), 1)
    picker = jnp.zeros((rows, seqs), jnp.float32)
    for n in range(seqs):
        picker = jnp.where((pick_col == n) & (pick_row == slots[n]), 1.0, picker)
    picker = picker.astype(jnp.bfloat16)

    column0 = my_v * width
    excess_sum = zero
    for n in range(seqs):
        loads[seqs + n].wait()
        spot = jnp.zeros((depth, LANES), jnp.int32)
        for j in range(depth):
            spot = jnp.where(sub == j, tok[n, j], spot)
        spot = spot - column0 - lane

        def pick(base, count, c, n=n, spot=spot):
            c = list(c)
            for k in range(count):
                hit = spot == (base + k) * LANES
                c[0] = jnp.where(hit, x[n, :, lane_tile(base + k)].astype(jnp.float32), c[0])
                c[1] = jnp.where(hit, d[n, :, lane_tile(base + k)].astype(jnp.float32), c[1])
            return tuple(c)

        first = (zero, zero)
        if tail:
            hit = (spot == full * LANES) & (lane < tail)
            first = (jnp.where(hit, tail_tile(x, n, 0.0), zero), jnp.where(hit, tail_tile(d, n, 0.0), zero))
        c = sweep(0, full, pick, first)
        excess_sum = jnp.where(lane == seqs + n, jnp.sum(c[0], axis=1, keepdims=True), excess_sum)
        excess_sum = jnp.where(lane == 2 * seqs + n, jnp.sum(c[1], axis=1, keepdims=True), excess_sum)

    arrive(stat_in, stat_ssem, stat_rsem)
    parts = [stat_in[p] for p in range(vocab)]
    peaks = [pltpu.roll(part, LANES - seqs, 1) for part in parts]
    peak_all = functools.reduce(jnp.maximum, peaks)
    merged = zero
    for part, local_peak in zip(parts, peaks):
        merged = merged + part * jnp.exp(local_peak - peak_all)
    scale = jnp.exp(tops - peak_all) / merged

    for n in range(seqs):
        scale_n = jnp.broadcast_to(scale[:, n:n + 1], (depth, LANES))

        def gap(base, count, c, n=n, scale_n=scale_n):
            c = list(c)
            for k in range(count):
                place = (base + k, pl.ds(n * depth, depth), slice(None))
                target = e[place] * scale_n
                over = jnp.maximum(target - d[n, :, lane_tile(base + k)].astype(jnp.float32), 0.0)
                e[place] = over + mixing * target
                c[k % 4] = c[k % 4] + over
            return tuple(c)

        first = zero
        if tail:
            place = (full, pl.ds(n * depth, depth), slice(None))
            target = e[place] * scale_n
            first = jnp.maximum(target - tail_tile(d, n, 0.0), 0.0)
            e[place] = first + mixing * target
        c = sweep(0, full, gap, (first, zero, zero, zero))
        total = jnp.sum((c[0] + c[1]) + (c[2] + c[3]), axis=1, keepdims=True)
        excess_sum = jnp.where(lane == n, total, excess_sum)

    spread_in[my_v] = excess_sum
    spread_copies = exchange(spread_in, spr_ssem, spr_rsem)

    arrive(spread_in, spr_ssem, spr_rsem)
    spread = spread_in[0]
    for p in range(1, vocab):
        spread = spread + spread_in[p]
    chosen = pltpu.roll(spread, LANES - seqs, 1)
    drafted = pltpu.roll(spread, LANES - 2 * seqs, 1)
    safe_draft = jnp.where(live, drafted, 1.0)
    accept = jnp.where(live, jnp.minimum(1.0, jnp.exp(chosen - peak_all) / merged / safe_draft), 0.0)
    before = []
    running = jnp.ones((1, LANES), jnp.float32)
    expected = jnp.zeros((1, LANES), jnp.float32)
    for j in range(depth):
        before.append(running)
        running = running * accept[j:j + 1, :]
        expected = expected + running
    before = jnp.concatenate(before, axis=0)
    weight = jnp.where(live, before * (1.0 - accept), 0.0)

    coef = weight / (spread + mixing)
    diag = lax.broadcasted_iota(jnp.int32, (seqs, LANES), 0) == lax.broadcasted_iota(jnp.int32, (seqs, LANES), 1)
    coefs = []
    for j in range(depth):
        row = jnp.where(diag, jnp.broadcast_to(coef[j:j + 1, :], (seqs, LANES)), 0.0)
        coefs.append(jnp.broadcast_to(jnp.sum(row, axis=1, keepdims=True), (seqs, LANES)))

    routed = []
    own_copies = []
    bounds = [tiles * c // CHUNKS for c in range(CHUNKS + 1)]
    for c in range(CHUNKS):
        def mix(base, count, carry):
            pieces = []
            for k in range(count):
                total = e[base + k, pl.ds(0, seqs, stride=depth), :] * coefs[0]
                for j in range(1, depth):
                    total = total + e[base + k, pl.ds(j, seqs, stride=depth), :] * coefs[j]
                pieces.append(total)
            mixed = pieces[0] if count == 1 else jnp.concatenate(pieces, axis=1)
            sent = jnp.dot(picker, mixed.astype(jnp.bfloat16), preferred_element_type=jnp.float32)
            columns = pl.ds(pl.multiple_of(base * LANES, LANES), count * LANES)
            for g in range(groups):
                send[g, :, columns] = sent[g * capacity:(g + 1) * capacity, :].astype(jnp.bfloat16)
            return carry

        sweep(bounds[c], bounds[c + 1], mix, 0, MIX_GROUP)
        columns = pl.ds(bounds[c] * LANES, (bounds[c + 1] - bounds[c]) * LANES)
        for k in range(1, groups):
            to = lax.rem(my_dp + k, groups)
            routed.append(pltpu.make_async_remote_copy(
                src_ref=send.at[to, :, columns], dst_ref=landed.at[my_dp, :, columns],
                send_sem=out_ssem.at[c, k], recv_sem=out_rsem.at[c, my_dp],
                device_id=(to, my_v), device_id_type=MESH,
            ))
            routed[-1].start()
        own_copies.append(pltpu.make_async_copy(
            send.at[my_dp, :, columns], landed.at[my_dp, :, columns], local_sem.at[c]))
        own_copies[-1].start()

    sent_accept = zero
    sent_expected = zero
    expected = jnp.broadcast_to(expected, (depth, LANES))
    for n in range(seqs):
        at_slot = lane == slots[n]
        sent_accept = jnp.where(at_slot, accept[:, n:n + 1], sent_accept)
        sent_expected = jnp.where(at_slot, expected[:, n:n + 1], sent_expected)
    for g in range(groups):
        shift = (LANES - g * capacity) % LANES
        small[g, 0:depth, :] = pltpu.roll(sent_accept, shift, 1) if shift else sent_accept
        small[g, depth:2 * depth, :] = pltpu.roll(sent_expected, shift, 1) if shift else sent_expected
    for k in range(1, groups):
        to = lax.rem(my_dp + k, groups)
        routed.append(pltpu.make_async_remote_copy(
            src_ref=small.at[to], dst_ref=small_in.at[my_dp],
            send_sem=sm_ssem.at[k], recv_sem=sm_rsem.at[my_dp],
            device_id=(to, my_v), device_id_type=MESH,
        ))
        routed[-1].start()
    stores = []
    for c in range(CHUNKS):
        columns = pl.ds(bounds[c] * LANES, (bounds[c + 1] - bounds[c]) * LANES)
        for k in range(1, groups):
            source = lax.rem(my_dp + k, groups)
            pltpu.make_async_remote_copy(
                src_ref=send.at[source, :, columns], dst_ref=landed.at[source, :, columns],
                send_sem=out_ssem.at[c, k], recv_sem=out_rsem.at[c, source],
                device_id=(source, my_v), device_id_type=MESH,
            ).wait_recv()
        own_copies[c].wait()

        def gather(base, count, carry):
            span = pl.ds(pl.multiple_of(base * LANES, LANES), count * LANES)
            pieces = [landed[g, :, span].astype(jnp.float32) for g in range(groups)]
            block[:, span] = jnp.concatenate(pieces, axis=0).astype(jnp.bfloat16)
            return carry

        sweep(bounds[c], bounds[c + 1], gather, 0, MIX_GROUP)
        stores.append(pltpu.make_async_copy(block.at[:, columns], out.at[:, columns], store_sem.at[c]))
        stores[-1].start()
    small_in[my_dp] = small[my_dp]
    for k in range(1, groups):
        source = lax.rem(my_dp + k, groups)
        pltpu.make_async_remote_copy(
            src_ref=small.at[source], dst_ref=small_in.at[source],
            send_sem=sm_ssem.at[k], recv_sem=sm_rsem.at[source],
            device_id=(source, my_v), device_id_type=MESH,
        ).wait_recv()
    final_accept = zero
    final_expected = zero
    for g in range(groups):
        mine = (lane >= g * capacity) & (lane < (g + 1) * capacity)
        final_accept = jnp.where(mine, pltpu.roll(small_in[g, 0:depth, :], g * capacity, 1), final_accept)
        final_expected = jnp.where(mine, pltpu.roll(small_in[g, depth:2 * depth, :], g * capacity, 1), final_expected)
    accept_out[...] = final_accept[:, :rows]
    expected_out[...] = final_expected[0:1, :rows]
    for copy in stores:
        copy.wait()
    for copy in stat_copies + spread_copies + routed:
        copy.wait_send()


def body(logits, draft_probs, draft_tokens, draft_lengths, owner_group):
    groups = lax.axis_size("dp")
    vocab = lax.axis_size("vocab")
    seqs, depth, width = logits.shape
    capacity = max(2, 2 * seqs // groups)
    tiles = -(-width // LANES)
    padded = tiles * LANES
    anywhere = pl.BlockSpec(memory_space=pl.ANY)
    hbm = pl.BlockSpec(memory_space=pltpu.HBM)
    dma = pltpu.SemaphoreType.DMA
    slots = groups * capacity
    vmem = pl.BlockSpec(memory_space=pltpu.VMEM)
    out, accept, expected = pl.pallas_call(
        functools.partial(kernel, (groups, vocab, capacity)),
        out_shape=(
            jax.ShapeDtypeStruct((slots, padded), jnp.bfloat16),
            jax.ShapeDtypeStruct((depth, slots), jnp.float32),
            jax.ShapeDtypeStruct((1, slots), jnp.float32),
        ),
        in_specs=[hbm] * 5,
        out_specs=(anywhere, vmem, vmem),
        scratch_shapes=[
            pltpu.SMEM((seqs, depth), jnp.int32),
            pltpu.SMEM((seqs,), jnp.int32),
            pltpu.SMEM((seqs,), jnp.int32),
            pltpu.VMEM((seqs, depth, width), jnp.bfloat16),
            pltpu.VMEM((seqs, depth, width), jnp.bfloat16),
            pltpu.VMEM((tiles, seqs * depth, LANES), jnp.float32),
            pltpu.VMEM((groups, capacity, padded), jnp.bfloat16),
            pltpu.VMEM((groups, capacity, padded), jnp.bfloat16),
            pltpu.VMEM((slots, padded), jnp.bfloat16),
            pltpu.VMEM((vocab, depth, LANES), jnp.float32),
            pltpu.VMEM((vocab, depth, LANES), jnp.float32),
            pltpu.VMEM((groups, 2 * depth, LANES), jnp.float32),
            pltpu.VMEM((groups, 2 * depth, LANES), jnp.float32),
            dma((3,)),
            dma((2 * seqs,)),
            dma((vocab,)),
            dma((vocab,)),
            dma((vocab,)),
            dma((vocab,)),
            dma((CHUNKS, groups)),
            dma((CHUNKS, groups)),
            dma((groups,)),
            dma((groups,)),
            dma((CHUNKS,)),
            dma((CHUNKS,)),
        ],
        compiler_params=pltpu.CompilerParams(
            collective_id=0, has_side_effects=True, vmem_limit_bytes=54500 * 1024
        ),
    )(draft_tokens, draft_lengths, owner_group, logits, draft_probs)
    correction = out[:, :width]
    accept_ratio = accept.T
    expected_accepted = expected.reshape(slots)
    return (correction, accept_ratio, expected_accepted)


def solution(mesh):
    placed = (P("dp", None, "vocab"), P("dp", None, "vocab"), P("dp", None), P("dp"), P("dp"))
    return jax.shard_map(
        body,
        mesh=mesh,
        in_specs=placed,
        out_specs=(P("dp", "vocab"), P("dp", None), P("dp")),
        check_vma=False,
    )
```

profile of v0, /device:TPU:0, one launch (start us, length us, event | category | flops | bytes accessed | tf_op | source)
XLA Modules:
  0.0 33.5 jit_solution(1574349809148313866)
XLA Ops:
  0.6 0.0 copy-start
  0.6 0.7 %copy-done = s32[8,8]{1,0:T(8,128)S(1)} copy-done((s32[8,8]{1,0:T(8,128)S(1)}, s32[8,8]{1,0:T(8,128)}, u32[]{:S(2)}) %copy-start) | copy-done | bytes 280
  1.3 0.0 copy-start.1
  1.3 0.7 %copy-done.1 = s32[8]{0:T(128)S(1)} copy-done((s32[8]{0:T(128)S(1)}, s32[8]{0:T(128)}, u32[]{:S(2)}) %copy-start.1) | copy-done | bytes 56
  2.0 0.0 copy-start.2
  2.0 0.7 %copy-done.2 = s32[8]{0:T(128)S(1)} copy-done((s32[8]{0:T(128)S(1)}, s32[8]{0:T(128)}, u32[]{:S(2)}) %copy-start.2) | copy-done | bytes 56
  2.6 28.9 %shard_map.76 = (bf16[16,19072]{1,0:T(8,128)(2,1)S(1)}, f32[8,16]{1,0:T(8,128)S(1)}, f32[1,16]{1,0:T(1,128)S(1)}) custom-call(s32[8,8]{1,0:T(8,128)S(1)} %copy-done, s32[8]{0:T(128)S(1)} %copy-done.1, s32[8]{0:T(128)S(1)} %copy-done.2, bf16[8,8,19008]{2,1,0:T(8,128)(2,1)} %x_hbm.1, bf16[8,8,19008]{2,1,0:T(8,128)(2,1)} %d_hbm.1), custom_call_target="tpu_custom_call" | custom-call | tf_op jit(solution)/shard_map/pallas_call | solution.py:357
  31.6 0.8 %copy.11 = bf16[16,19008]{1,0:T(8,128)(2,1)} copy(bf16[16,19008]{1,0:T(8,128)(2,1)S(1)} %bitcast.3) | data formatting | bytes 1216512
  32.4 0.6 %copy.12 = f32[16,8]{0,1:T(8,128)} copy(f32[16,8]{0,1:T(8,128)S(1)} %bitcast.4) | data formatting | bytes 1024
  33.0 0.5 %copy.13 = f32[16]{0:T(128)} copy(f32[16]{0:T(128)S(1)} %bitcast.5) | data formatting | bytes 128
Async XLA Ops:
  0.6 0.7 %copy-start = (s32[8,8]{1,0:T(8,128)S(1)}, s32[8,8]{1,0:T(8,128)}, u32[]{:S(2)}) copy-start(s32[8,8]{1,0:T(8,128)} %tok_hbm.1) | copy-start | bytes 772
  1.3 0.7 %copy-start.1 = (s32[8]{0:T(128)S(1)}, s32[8]{0:T(128)}, u32[]{:S(2)}) copy-start(s32[8]{0:T(128)} %lens_hbm.1) | copy-start | bytes 100
  2.0 0.7 %copy-start.2 = (s32[8]{0:T(128)S(1)}, s32[8]{0:T(128)}, u32[]{:S(2)}) copy-start(s32[8]{0:T(128)} %own_hbm.1) | copy-start | bytes 100
where the time goes:
time: 33.7 us; the launch traced here: 33.5 us
  Pallas kernels  28.9 us (86%)
  local copies, waits for them, and re-layouts  3.92 us (12%)
  between operations  0.65 us (2%)
    pallas_call x1, Pallas kernels, body(): pl.pallas_call(functools.partial(kernel, (groups, vocab, capacity)), out_...  28.9 us
    unnamed x9, local copies, waits for them, and re-layouts  3.92 us

commit v1 on v0

v1 whole, which is shorter than its diff:
```python
import functools

import jax
import jax.numpy as jnp
from jax import lax
from jax.experimental import pallas as pl
from jax.experimental.pallas import tpu as pltpu
from jax.sharding import PartitionSpec as P

mixing = 0.1
LANES = 128
SLAB = 8
PIECE = 2
BATCHES = 1
TERMS = 3
PAIR = 2
FIRST = 6
GROWTH = 3
MOST = 40
LOW = -1e30
MESH = pl.DeviceIdType.MESH
scope = jax.named_scope


def slabs(full, size):
    return [(a, min(size, full - a)) for a in range(0, full, size)]


def plan(tiles):
    bounds, size = [0], FIRST
    while bounds[-1] < tiles:
        bounds.append(min(tiles, bounds[-1] + size))
        size = min(size * GROWTH, MOST)
    return bounds


def xor(value, mask):
    bit = 1
    while bit <= mask:
        if mask & bit:
            value = value + bit - 2 * bit * lax.rem(value // bit, 2)
        bit *= 2
    return value


def partners(me, count):
    if count & (count - 1):
        return [lax.rem(me + k, count) for k in range(1, count)]
    return [xor(me, k) for k in range(count - 1, 0, -1)]


def tree(op, values):
    values = list(values)
    while len(values) > 1:
        values = [op(*values[i:i + 2]) if i + 1 < len(values) else values[i] for i in range(0, len(values), 2)]
    return values[0]


def kernel(
    dims,
    tok_hbm, lens_hbm, own_hbm, x_hbm, d_hbm,
    block, accept_out, expected_out,
    tok, lens, own, x, d, e, send, landed, comm, small, small_in,
    scalar_sem, x_sem, d_sem, comm_ssem, comm_rsem, out_ssem, out_rsem, sm_ssem, sm_rsem,
):
    groups, vocab, capacity = dims
    seqs, depth, width = x_hbm.shape
    full = width // LANES
    tail = width - full * LANES
    tiles = e.shape[2] // LANES
    rows = seqs * depth
    slots = groups * capacity
    half = LANES // 2
    pick_slot, norm_slot = BATCHES, BATCHES + 1
    my_dp = lax.axis_index("dp")
    my_v = lax.axis_index("vocab")

    pairs = slabs(seqs, PAIR)
    x_loads, d_loads = [], []
    for i, (n, size) in enumerate(pairs):
        part = pl.ds(n, size)
        x_loads.append(pltpu.make_async_copy(x_hbm.at[part], x.at[part], x_sem.at[i]))
        d_loads.append(pltpu.make_async_copy(d_hbm.at[part], d.at[part], d_sem))
        x_loads[-1].start()
    scalars = []
    for i, (source, target) in enumerate(((tok_hbm, tok), (lens_hbm, lens), (own_hbm, own))):
        scalars.append(pltpu.make_async_copy(source, target, scalar_sem.at[i]))
        scalars[-1].start()

    barrier = pltpu.get_barrier_semaphore()
    v_peers = [lax.rem(my_v + k, vocab) for k in range(1, vocab)]
    g_peers = partners(my_dp, groups)
    for p in v_peers:
        pl.semaphore_signal(barrier, inc=1, device_id=(my_dp, p), device_id_type=MESH)
    for p in g_peers:
        pl.semaphore_signal(barrier, inc=1, device_id=(p, my_v), device_id_type=MESH)

    sub = lax.broadcasted_iota(jnp.int32, (depth, LANES), 0)
    lane = lax.broadcasted_iota(jnp.int32, (depth, LANES), 1)
    row_lane = lax.broadcasted_iota(jnp.int32, (1, LANES), 1)
    lane_j = lax.rem(row_lane, depth)
    lane_n = lax.rem(row_lane // depth, seqs)
    zero = jnp.zeros((depth, LANES), jnp.float32)
    spots = [(lax.rem(lane, depth) == sub) & (lax.rem(lane // depth, seqs) == n) for n in range(seqs)]

    def tail_tile(ref, n, fill):
        part = ref[n, :, pl.ds(full * LANES, tail)].astype(jnp.float32)
        return jnp.concatenate([part, jnp.full((depth, LANES - tail), fill, jnp.float32)], axis=1)

    def to_row(columns):
        spread = zero
        for n, column in columns.items():
            spread = jnp.where(spots[n], column, spread)
        return jnp.sum(spread, axis=0, keepdims=True)

    def to_column(row, n):
        placed = jnp.where(spots[n] & (lane < rows), row, 0.0)
        return jnp.sum(placed, axis=1, keepdims=True)

    def exchange(slot):
        for to in v_peers:
            pltpu.make_async_remote_copy(
                src_ref=comm.at[slot, my_v], dst_ref=comm.at[slot, my_v],
                send_sem=comm_ssem, recv_sem=comm_rsem.at[slot],
                device_id=(my_dp, to), device_id_type=MESH,
            ).start()

    def arrive(slot):
        others = comm.at[slot, pl.ds(0, vocab - 1)]
        pltpu.make_async_remote_copy(
            src_ref=others, dst_ref=others, send_sem=comm_ssem, recv_sem=comm_rsem.at[slot],
            device_id=(my_dp, v_peers[0]), device_id_type=MESH,
        ).wait_recv()

    def peak(n):
        wide = 2 * LANES
        running = [x[n, :, pl.ds(k * wide, wide)] for k in range(min(4, full // 2))]
        for k in range(4, full // 2):
            running[k % 4] = jnp.maximum(running[k % 4], x[n, :, pl.ds(k * wide, wide)])
        top = tree(jnp.maximum, running).astype(jnp.float32)
        top = jnp.maximum(top[:, :LANES], top[:, LANES:])
        if full % 2:
            top = jnp.maximum(top, x[n, :, pl.ds((full - 1) * LANES, LANES)].astype(jnp.float32))
        if tail:
            top = jnp.maximum(top, tail_tile(x, n, LOW))
        return jnp.max(top, axis=1, keepdims=True)

    def expo(n, top):
        parts = [zero] * 4
        for a, size in slabs(full, SLAB):
            raw = x[n, :, pl.ds(a * LANES, size * LANES)].astype(jnp.float32)
            value = jnp.exp(raw - top)
            e[n, :, pl.ds(a * LANES, size * LANES)] = value
            for k in range(size):
                parts[k % 4] = parts[k % 4] + value[:, k * LANES:(k + 1) * LANES]
        if tail:
            value = jnp.exp(tail_tile(x, n, LOW) - top)
            e[n, :, pl.ds(full * LANES, LANES)] = value
            parts[0] = parts[0] + value
        return jnp.sum((parts[0] + parts[1]) + (parts[2] + parts[3]), axis=1, keepdims=True)

    tops, sums = {}, {}

    def take(i):
        n, size = pairs[i]
        with scope(f"load{i}"):
            x_loads[i].wait()
            if i == 0:
                for load in d_loads:
                    load.start()
        with scope(f"peak{i}"):
            for m in range(n, n + size):
                tops[m] = peak(m)

    take(0)
    for i, (n, size) in enumerate(pairs):
        if i + 1 < len(pairs):
            take(i + 1)
        with scope(f"expo{i}"):
            for m in range(n, n + size):
                sums[m] = expo(m, tops[m])
    with scope("send1"):
        comm[0, my_v] = jnp.concatenate([to_row(tops), to_row(sums)], axis=0)
    with scope("barrier"):
        pl.semaphore_wait(barrier, vocab - 1 + groups - 1)
        exchange(0)

    with scope("pick"):
        column0 = my_v * width
        chosen, drafted = {}, {}
        for copy in scalars:
            copy.wait()
        pltpu.make_async_copy(d_hbm, d, d_sem).wait()
        for n in range(seqs):
            spot = jnp.zeros((depth, LANES), jnp.int32)
            for j in range(depth):
                spot = jnp.where(sub == j, tok[n, j], spot)
            spot = spot - column0 - lane
            hit_x, hit_d = zero, zero
            if tail:
                hit = (spot == full * LANES) & (lane < tail)
                hit_x = jnp.where(hit, tail_tile(x, n, 0.0), hit_x)
                hit_d = jnp.where(hit, tail_tile(d, n, 0.0), hit_d)
            for a, size in slabs(full, SLAB):
                columns = pl.ds(a * LANES, size * LANES)
                raw_x, raw_d = x[n, :, columns].astype(jnp.float32), d[n, :, columns].astype(jnp.float32)
                for k in range(size):
                    hit = spot == (a + k) * LANES
                    hit_x = jnp.where(hit, raw_x[:, k * LANES:(k + 1) * LANES], hit_x)
                    hit_d = jnp.where(hit, raw_d[:, k * LANES:(k + 1) * LANES], hit_d)
            chosen[n] = jnp.sum(hit_x, axis=1, keepdims=True)
            drafted[n] = jnp.sum(hit_d, axis=1, keepdims=True)
        comm[pick_slot, my_v] = jnp.concatenate([to_row(chosen), to_row(drafted)], axis=0)
        exchange(pick_slot)

    with scope("arrive1"):
        arrive(0)
    with scope("merge"):
        parts = [comm[0, p] for p in range(vocab)]
        peak_row = tree(jnp.maximum, [part[0:1] for part in parts])
        total_row = tree(jnp.add, [part[1:2] * jnp.exp(part[0:1] - peak_row) for part in parts])
        scale = jnp.exp(comm[0, my_v][0:1] - peak_row) / total_row
        scales = {n: to_column(scale, n) for n in range(seqs)}
    norms = {}
    for n in range(seqs):
        with scope(f"gap{n}"):
            upper = scales[n] * (1.0 + mixing)
            lower = scales[n] * mixing
            parts = [zero] * 4
            for a, size in slabs(full, SLAB):
                columns = pl.ds(a * LANES, size * LANES)
                value = e[n, :, columns]
                value = jnp.maximum(value * upper - d[n, :, columns].astype(jnp.float32), value * lower)
                e[n, :, columns] = value
                for k in range(size):
                    parts[k % 4] = parts[k % 4] + value[:, k * LANES:(k + 1) * LANES]
            if tail:
                value = e[n, :, pl.ds(full * LANES, LANES)]
                value = jnp.maximum(value * upper - tail_tile(d, n, 0.0), value * lower)
                e[n, :, pl.ds(full * LANES, LANES)] = value
                parts[0] = parts[0] + value
            norms[n] = jnp.sum((parts[0] + parts[1]) + (parts[2] + parts[3]), axis=1, keepdims=True)
    with scope("send2"):
        norm = to_row(norms)
        comm[norm_slot, my_v] = jnp.concatenate([norm, norm], axis=0)
        exchange(norm_slot)

    with scope("arrivep"):
        arrive(pick_slot)
    with scope("weights"):
        picked = tree(jnp.add, [comm[pick_slot, p] for p in range(vocab)])
        length_row = jnp.zeros((1, LANES), jnp.int32)
        places = []
        for n in range(seqs):
            rank = jnp.int32(0)
            for i in range(n):
                rank = rank + jnp.where(own[i] == own[n], 1, 0)
            places.append(own[n] * capacity + rank)
            length_row = jnp.where(lane_n == n, lens[n], length_row)
        live = lane_j < length_row
        safe_draft = jnp.where(live, picked[1:2], 1.0)
        accept = jnp.where(live, jnp.minimum(1.0, jnp.exp(picked[0:1] - peak_row) / total_row / safe_draft), 0.0)
        wide = jnp.broadcast_to(accept, (depth, LANES))
        before = tree(jnp.multiply, [
            jnp.where(lane_j >= k, pltpu.roll(wide, k, 1)[0:1], 1.0) for k in range(1, depth)
        ])
        weight = jnp.where(live, before * (1.0 - accept), 0.0)
        survive = before * accept
        inner = lax.broadcasted_iota(jnp.int32, (slots, TERMS * rows), 1)
        outer = lax.broadcasted_iota(jnp.int32, (slots, TERMS * rows), 0)
        picker = jnp.zeros((slots, TERMS * rows), jnp.float32)
        for n in range(seqs):
            picker = jnp.where((lax.rem(inner // depth, seqs) == n) & (outer == places[n]), 1.0, picker)
        picker = picker.astype(jnp.bfloat16)
    with scope("smallsend"):
        sent = zero
        for n in range(seqs):
            sent = jnp.where(lane == places[n], to_column(accept, n), sent)
            alive = jnp.where((lane_n == n) & (row_lane < rows), survive, 0.0)
            sent = jnp.where(lane == places[n] + half, jnp.sum(alive, axis=1, keepdims=True), sent)
        for g in range(groups):
            shift = (LANES - g * capacity) % LANES
            small[g] = pltpu.roll(sent, shift, 1) if shift else sent
        for to in g_peers:
            pltpu.make_async_remote_copy(
                src_ref=small.at[to], dst_ref=small_in.at[my_dp], send_sem=sm_ssem, recv_sem=sm_rsem,
                device_id=(to, my_v), device_id_type=MESH,
            ).start()
        small_in[my_dp] = small[my_dp]

    with scope("arrive2"):
        arrive(norm_slot)
    with scope("coef"):
        coef = weight / tree(jnp.add, [comm[norm_slot, p][0:1] for p in range(vocab)])
        coefs = [to_column(coef, n) for n in range(seqs)]

    bounds = plan(tiles)
    chunks = len(bounds) - 1

    def span(c):
        return pl.ds(bounds[c] * LANES, (bounds[c + 1] - bounds[c]) * LANES)

    for c in range(chunks):
        with scope(f"mix{c}"):
            for a, size in slabs(bounds[c + 1] - bounds[c], PIECE):
                columns = pl.ds((bounds[c] + a) * LANES, size * LANES)
                value = jnp.concatenate([e[n, :, columns] * coefs[n] for n in range(seqs)], axis=0)
                terms = []
                for _ in range(TERMS):
                    terms.append(value.astype(jnp.bfloat16))
                    value = value - terms[-1].astype(jnp.float32)
                mixed = jnp.dot(picker, jnp.concatenate(terms, axis=0), preferred_element_type=jnp.float32)
                for g in range(groups):
                    send[g, :, columns] = mixed[g * capacity:(g + 1) * capacity].astype(jnp.bfloat16)
            for to in g_peers:
                pltpu.make_async_remote_copy(
                    src_ref=send.at[to, :, span(c)], dst_ref=landed.at[my_dp, :, span(c)],
                    send_sem=out_ssem, recv_sem=out_rsem.at[c],
                    device_id=(to, my_v), device_id_type=MESH,
                ).start()
            landed[my_dp, :, span(c)] = send[my_dp, :, span(c)]

    with scope("smallrecv"):
        others = pl.ds(0, groups - 1)
        pltpu.make_async_remote_copy(
            src_ref=small.at[others], dst_ref=small_in.at[others], send_sem=sm_ssem, recv_sem=sm_rsem,
            device_id=(g_peers[0], my_v), device_id_type=MESH,
        ).wait()
        final = zero
        for g in range(groups):
            mine = lax.rem(lane, half) // capacity == g
            final = jnp.where(mine, pltpu.roll(small_in[g], g * capacity, 1), final)
        accept_out[...] = final[:, :slots]
        expected_out[...] = final[0:1, half:half + slots]

    for c in range(chunks):
        with scope(f"recv{c}"):
            pltpu.make_async_remote_copy(
                src_ref=send.at[others, :, span(c)], dst_ref=landed.at[others, :, span(c)],
                send_sem=out_ssem, recv_sem=out_rsem.at[c],
                device_id=(g_peers[0], my_v), device_id_type=MESH,
            ).wait_recv()
        with scope(f"gather{c}"):
            for a, size in slabs(bounds[c + 1] - bounds[c], SLAB):
                start = (bounds[c] + a) * LANES
                columns = pl.ds(start, size * LANES)
                pieces = [landed[g, :, columns].astype(jnp.float32) for g in range(groups)]
                whole = jnp.concatenate(pieces, axis=0).astype(jnp.bfloat16)
                kept = min(size * LANES, width - start)
                block[:, pl.ds(start, kept)] = whole[:, :kept]
    with scope("sendwait"):
        pltpu.make_async_remote_copy(
            src_ref=send.at[others], dst_ref=landed.at[others], send_sem=out_ssem, recv_sem=out_rsem.at[0],
            device_id=(g_peers[0], my_v), device_id_type=MESH,
        ).wait_send()
        others = comm.at[:, pl.ds(0, vocab - 1)]
        pltpu.make_async_remote_copy(
            src_ref=others, dst_ref=others, send_sem=comm_ssem, recv_sem=comm_rsem.at[0],
            device_id=(my_dp, v_peers[0]), device_id_type=MESH,
        ).wait_send()


def finish(block, accept, expected, out, accept_out, expected_out, sem):
    pairs = ((block, out), (accept, accept_out), (expected, expected_out))
    copies = [pltpu.make_async_copy(a, b, sem.at[i]) for i, (a, b) in enumerate(pairs)]
    for copy in copies:
        copy.start()
    for copy in copies:
        copy.wait()


def body(logits, draft_probs, draft_tokens, draft_lengths, owner_group):
    groups = lax.axis_size("dp")
    vocab = lax.axis_size("vocab")
    seqs, depth, width = logits.shape
    capacity = max(2, 2 * seqs // groups)
    tiles = -(-width // LANES)
    padded = tiles * LANES
    chunks = len(plan(tiles)) - 1
    hbm = pl.BlockSpec(memory_space=pltpu.HBM)
    vmem = pl.BlockSpec(memory_space=pltpu.VMEM)
    dma = pltpu.SemaphoreType.DMA
    slots = groups * capacity
    shapes = (
        jax.ShapeDtypeStruct((slots, width), jnp.bfloat16),
        jax.ShapeDtypeStruct((depth, slots), jnp.float32),
        jax.ShapeDtypeStruct((1, slots), jnp.float32),
    )
    outs = pl.pallas_call(
        functools.partial(kernel, (groups, vocab, capacity)),
        out_shape=shapes,
        in_specs=[hbm] * 5,
        out_specs=(vmem, vmem, vmem),
        scratch_shapes=[
            pltpu.SMEM((seqs, depth), jnp.int32),
            pltpu.SMEM((seqs,), jnp.int32),
            pltpu.SMEM((seqs,), jnp.int32),
            pltpu.VMEM((seqs, depth, width), jnp.bfloat16),
            pltpu.VMEM((seqs, depth, width), jnp.bfloat16),
            pltpu.VMEM((seqs, depth, padded), jnp.float32),
            pltpu.VMEM((groups, capacity, padded), jnp.bfloat16),
            pltpu.VMEM((groups, capacity, padded), jnp.bfloat16),
            pltpu.VMEM((BATCHES + 2, vocab, 2, LANES), jnp.float32),
            pltpu.VMEM((groups, depth, LANES), jnp.float32),
            pltpu.VMEM((groups, depth, LANES), jnp.float32),
            dma((3,)),
            dma((len(slabs(seqs, PAIR)),)),
            dma(()),
            dma(()),
            dma((BATCHES + 2,)),
            dma(()),
            dma((chunks,)),
            dma(()),
            dma(()),
        ],
        compiler_params=pltpu.CompilerParams(
            collective_id=0, has_side_effects=True, vmem_limit_bytes=54500 * 1024
        ),
    )(*[pltpu.with_memory_space_constraint(a, pltpu.HBM) for a in (draft_tokens, draft_lengths, owner_group)], logits, draft_probs)
    out, accept, expected = pl.pallas_call(
        finish,
        out_shape=shapes,
        in_specs=[vmem] * 3,
        out_specs=(hbm, hbm, hbm),
        scratch_shapes=[dma((3,))],
        compiler_params=pltpu.CompilerParams(vmem_limit_bytes=1024 * 1024),
    )(*outs)
    return (out, accept.T, expected.reshape(slots))


def solution(mesh):
    placed = (P("dp", None, "vocab"), P("dp", None, "vocab"), P("dp", None), P("dp"), P("dp"))
    return jax.shard_map(
        body,
        mesh=mesh,
        in_specs=placed,
        out_specs=(P("dp", "vocab"), P("dp", None), P("dp")),
        check_vma=False,
    )
```

time: 33.7 us -> 25.6 us (0.76)
  Pallas kernels: 28.9 us -> 24.8 us
  local copies, waits for them, and re-layouts: 3.92 us -> 0 us
    pallas_call x1, Pallas kernels: 28.9 us -> 23.9 us  [body(): pl.pallas_call(functools.partial(kernel, (groups, vocab, capacity)), out_...]
    unnamed x9 -> x0, local copies, waits for them, and re-layouts: 3.92 us -> none
    pallas_call x0 -> x1, Pallas kernels: none -> 0.85 us  [body(): pl.pallas_call(finish, out_shape=shapes, in_specs=[vmem] * 3, out_specs=(...]
where the time goes in v1:
time: 25.6 us; the launch traced here: 25.4 us
  Pallas kernels  24.8 us (97%)
  between operations  0.64 us (2%)
    pallas_call x1, Pallas kernels, body(): pl.pallas_call(functools.partial(kernel, (groups, vocab, capacity)), out_...  23.9 us
    pallas_call x1, Pallas kernels, body(): pl.pallas_call(finish, out_shape=shapes, in_specs=[vmem] * 3, out_specs=(...  0.85 us

profile of v1, /device:TPU:0, one launch (start us, length us, event | category | flops | bytes accessed | tf_op | source)
XLA Modules:
  0.0 25.4 jit_solution(4559112051394699232)
XLA Ops:
  0.6 23.9 %shard_map.76 = (bf16[16,19008]{1,0:T(8,128)(2,1)S(1)}, f32[8,16]{1,0:T(8,128)S(1)}, f32[1,16]{1,0:T(1,128)S(1)}) custom-call(s32[8,8]{1,0:T(8,128)} %tok_hbm.1, s32[8]{0:T(128)} %lens_hbm.1, s32[8]{0:T(128)} %own_hbm.1, bf16[8,8,19008]{2,1,0:T(8,128)(2,1)} %x_hbm.1, bf16[8,8,19008]{2,1,0:T(8,128)(2,1)} %d_hbm.1), custom_call_target="tpu_custom_call" | custom-call | tf_op jit(solution)/shard_map/pallas_call | solution.py:389
  24.6 0.9 %shard_map.77 = (bf16[16,19008]{1,0:T(8,128)(2,1)}, f32[8,16]{1,0:T(8,128)}, f32[1,16]{1,0:T(1,128)}) custom-call(bf16[16,19008]{1,0:T(8,128)(2,1)S(1)} %get-tuple-element.9.block, f32[8,16]{1,0:T(8,128)S(1)} %get-tuple-element.10.accept, f32[1,16]{1,0:T(1,128)S(1)} %get-tuple-element.11.expected), custom_call_target="tpu_custom_call" | custom-call | tf_op jit(solution)/shard_map/pallas_call | solution.py:420

commit v2 on v1

--- a/solution.py
+++ b/solution.py
@@ -13,8 +13,9 @@
 PIECE = 2
 BATCHES = 1
 TERMS = 3
+PARTS = 1
 PAIR = 2
-FIRST = 6
+FIRST = 4
 GROWTH = 3
 MOST = 40
 LOW = -1e30
@@ -47,6 +48,11 @@
     if count & (count - 1):
         return [lax.rem(me + k, count) for k in range(1, count)]
     return [xor(me, k) for k in range(count - 1, 0, -1)]
+
+
+def by_distance(me, count):
+    picks = [jnp.where(2 * me < count, count - 2 - i, i) for i in range(count - 1)]
+    return [p + jnp.where(p >= me, 1, 0) for p in picks]
 
 
 def tree(op, values):
@@ -75,6 +81,14 @@
     my_dp = lax.axis_index("dp")
     my_v = lax.axis_index("vocab")
 
+    barrier = pltpu.get_barrier_semaphore()
+    v_peers = by_distance(my_v, vocab)
+    g_peers = partners(my_dp, groups)
+    for p in v_peers:
+        pl.semaphore_signal(barrier, inc=1, device_id=(my_dp, p), device_id_type=MESH)
+    for p in g_peers:
+        pl.semaphore_signal(barrier, inc=1, device_id=(p, my_v), device_id_type=MESH)
+
     pairs = slabs(seqs, PAIR)
     x_loads, d_loads = [], []
     for i, (n, size) in enumerate(pairs):
@@ -86,14 +100,6 @@
     for i, (source, target) in enumerate(((tok_hbm, tok), (lens_hbm, lens), (own_hbm, own))):
         scalars.append(pltpu.make_async_copy(source, target, scalar_sem.at[i]))
         scalars[-1].start()
-
-    barrier = pltpu.get_barrier_semaphore()
-    v_peers = [lax.rem(my_v + k, vocab) for k in range(1, vocab)]
-    g_peers = partners(my_dp, groups)
-    for p in v_peers:
-        pl.semaphore_signal(barrier, inc=1, device_id=(my_dp, p), device_id_type=MESH)
-    for p in g_peers:
-        pl.semaphore_signal(barrier, inc=1, device_id=(p, my_v), device_id_type=MESH)
 
     sub = lax.broadcasted_iota(jnp.int32, (depth, LANES), 0)
     lane = lax.broadcasted_iota(jnp.int32, (depth, LANES), 1)
@@ -187,7 +193,7 @@
 
     with scope("pick"):
         column0 = my_v * width
-        chosen, drafted = {}, {}
+        chosen, drafted, masses = {}, {}, {}
         for copy in scalars:
             copy.wait()
         pltpu.make_async_copy(d_hbm, d, d_sem).wait()
@@ -196,11 +202,12 @@
             for j in range(depth):
                 spot = jnp.where(sub == j, tok[n, j], spot)
             spot = spot - column0 - lane
-            hit_x, hit_d = zero, zero
+            hit_x, hit_d, mass = zero, zero, [zero] * 4
             if tail:
                 hit = (spot == full * LANES) & (lane < tail)
                 hit_x = jnp.where(hit, tail_tile(x, n, 0.0), hit_x)
                 hit_d = jnp.where(hit, tail_tile(d, n, 0.0), hit_d)
+                mass[0] = tail_tile(d, n, 0.0)
             for a, size in slabs(full, SLAB):
                 columns = pl.ds(a * LANES, size * LANES)
                 raw_x, raw_d = x[n, :, columns].astype(jnp.float32), d[n, :, columns].astype(jnp.float32)
@@ -208,8 +215,10 @@
                     hit = spot == (a + k) * LANES
                     hit_x = jnp.where(hit, raw_x[:, k * LANES:(k + 1) * LANES], hit_x)
                     hit_d = jnp.where(hit, raw_d[:, k * LANES:(k + 1) * LANES], hit_d)
+                    mass[k % 4] = mass[k % 4] + raw_d[:, k * LANES:(k + 1) * LANES]
             chosen[n] = jnp.sum(hit_x, axis=1, keepdims=True)
             drafted[n] = jnp.sum(hit_d, axis=1, keepdims=True)
+            masses[n] = (mass[0] + mass[1]) + (mass[2] + mass[3])
         comm[pick_slot, my_v] = jnp.concatenate([to_row(chosen), to_row(drafted)], axis=0)
         exchange(pick_slot)
 
@@ -219,29 +228,24 @@
         parts = [comm[0, p] for p in range(vocab)]
         peak_row = tree(jnp.maximum, [part[0:1] for part in parts])
         total_row = tree(jnp.add, [part[1:2] * jnp.exp(part[0:1] - peak_row) for part in parts])
-        scale = jnp.exp(comm[0, my_v][0:1] - peak_row) / total_row
-        scales = {n: to_column(scale, n) for n in range(seqs)}
-    norms = {}
+        mine = comm[0, my_v]
+        scale = jnp.exp(mine[0:1] - peak_row) / total_row
+        scales = [to_column(scale, n) for n in range(seqs)]
+    excess = {}
     for n in range(seqs):
         with scope(f"gap{n}"):
-            upper = scales[n] * (1.0 + mixing)
-            lower = scales[n] * mixing
             parts = [zero] * 4
             for a, size in slabs(full, SLAB):
                 columns = pl.ds(a * LANES, size * LANES)
-                value = e[n, :, columns]
-                value = jnp.maximum(value * upper - d[n, :, columns].astype(jnp.float32), value * lower)
-                e[n, :, columns] = value
+                upper = jnp.maximum(e[n, :, columns] * scales[n], d[n, :, columns].astype(jnp.float32))
                 for k in range(size):
-                    parts[k % 4] = parts[k % 4] + value[:, k * LANES:(k + 1) * LANES]
+                    parts[k % 4] = parts[k % 4] + upper[:, k * LANES:(k + 1) * LANES]
             if tail:
-                value = e[n, :, pl.ds(full * LANES, LANES)]
-                value = jnp.maximum(value * upper - tail_tile(d, n, 0.0), value * lower)
-                e[n, :, pl.ds(full * LANES, LANES)] = value
-                parts[0] = parts[0] + value
-            norms[n] = jnp.sum((parts[0] + parts[1]) + (parts[2] + parts[3]), axis=1, keepdims=True)
+                parts[0] = parts[0] + jnp.maximum(e[n, :, pl.ds(full * LANES, LANES)] * scales[n], tail_tile(d, n, 0.0))
+            total = (parts[0] + parts[1]) + (parts[2] + parts[3])
+            excess[n] = jnp.sum(total - masses[n], axis=1, keepdims=True)
     with scope("send2"):
-        norm = to_row(norms)
+        norm = to_row(excess) + mixing * scale * mine[1:2]
         comm[norm_slot, my_v] = jnp.concatenate([norm, norm], axis=0)
         exchange(norm_slot)
 
@@ -293,18 +297,40 @@
     with scope("coef"):
         coef = weight / tree(jnp.add, [comm[norm_slot, p][0:1] for p in range(vocab)])
         coefs = [to_column(coef, n) for n in range(seqs)]
+        lowers = [to_column(coef * scale * mixing, n) for n in range(seqs)]
+        uppers = [to_column(coef * scale * (1.0 + mixing), n) for n in range(seqs)]
 
     bounds = plan(tiles)
     chunks = len(bounds) - 1
 
+    def pieces(c):
+        whole = min(bounds[c + 1], full)
+        found = [(bounds[c] + a, size) for a, size in slabs(whole - bounds[c], PIECE)]
+        return found + ([(full, 1)] if bounds[c + 1] > full else [])
+
     def span(c):
         return pl.ds(bounds[c] * LANES, (bounds[c + 1] - bounds[c]) * LANES)
 
+    square = groups == 4
+    near, far, across = xor(my_dp, 1), xor(my_dp, 2), xor(my_dp, 3)
+
+    def ship(c, to):
+        pltpu.make_async_remote_copy(
+            src_ref=send.at[to, :, span(c)], dst_ref=landed.at[my_dp, :, span(c)],
+            send_sem=out_ssem, recv_sem=out_rsem.at[c],
+            device_id=(to, my_v), device_id_type=MESH,
+        ).start()
+
     for c in range(chunks):
         with scope(f"mix{c}"):
-            for a, size in slabs(bounds[c + 1] - bounds[c], PIECE):
-                columns = pl.ds((bounds[c] + a) * LANES, size * LANES)
-                value = jnp.concatenate([e[n, :, columns] * coefs[n] for n in range(seqs)], axis=0)
+            for start, size in pieces(c):
+                columns = pl.ds(start * LANES, size * LANES)
+                values = []
+                for n in range(seqs):
+                    value = e[n, :, columns]
+                    draft = tail_tile(d, n, 0.0) if start >= full else d[n, :, columns].astype(jnp.float32)
+                    values.append(jnp.maximum(value * uppers[n] - draft * coefs[n], value * lowers[n]))
+                value = jnp.concatenate(values, axis=0)
                 terms = []
                 for _ in range(TERMS):
                     terms.append(value.astype(jnp.bfloat16))
@@ -312,13 +338,31 @@
                 mixed = jnp.dot(picker, jnp.concatenate(terms, axis=0), preferred_element_type=jnp.float32)
                 for g in range(groups):
                     send[g, :, columns] = mixed[g * capacity:(g + 1) * capacity].astype(jnp.bfloat16)
-            for to in g_peers:
-                pltpu.make_async_remote_copy(
-                    src_ref=send.at[to, :, span(c)], dst_ref=landed.at[my_dp, :, span(c)],
-                    send_sem=out_ssem, recv_sem=out_rsem.at[c],
-                    device_id=(to, my_v), device_id_type=MESH,
-                ).start()
+            if square:
+                ship(c, far)
+
+                @pl.when(across < near)
+                def _():
+                    ship(c, across)
+
+                @pl.when(jnp.logical_not(across < near))
+                def _():
+                    ship(c, near)
+            else:
+                for to in g_peers:
+                    ship(c, to)
             landed[my_dp, :, span(c)] = send[my_dp, :, span(c)]
+
+    if square:
+        @pl.when(across < near)
+        def _():
+            for c in range(chunks):
+                ship(c, near)
+
+        @pl.when(jnp.logical_not(across < near))
+        def _():
+            for c in range(chunks):
+                ship(c, across)
 
     with scope("smallrecv"):
         others = pl.ds(0, groups - 1)
@@ -361,7 +405,9 @@
 
 
 def finish(block, accept, expected, out, accept_out, expected_out, sem):
-    pairs = ((block, out), (accept, accept_out), (expected, expected_out))
+    step = -(-block.shape[1] // (PARTS * LANES)) * LANES
+    spans = [pl.ds(a, min(step, block.shape[1] - a)) for a in range(0, block.shape[1], step)]
+    pairs = [(block.at[:, c], out.at[:, c]) for c in spans] + [(accept, accept_out), (expected, expected_out)]
     copies = [pltpu.make_async_copy(a, b, sem.at[i]) for i, (a, b) in enumerate(pairs)]
     for copy in copies:
         copy.start()
@@ -422,7 +468,7 @@
         out_shape=shapes,
         in_specs=[vmem] * 3,
         out_specs=(hbm, hbm, hbm),
-        scratch_shapes=[dma((3,))],
+        scratch_shapes=[dma((PARTS + 2,))],
         compiler_params=pltpu.CompilerParams(vmem_limit_bytes=1024 * 1024),
     )(*outs)
     return (out, accept.T, expected.reshape(slots))

time: 25.6 us -> 24.6 us (0.961)
  Pallas kernels: 24.8 us -> 23.8 us
    pallas_call x1, Pallas kernels: 23.9 us -> 23 us  [body(): pl.pallas_call(functools.partial(kernel, (groups, vocab, capacity)), out_...]
where the time goes in v2:
time: 24.6 us; the launch traced here: 24.5 us
  Pallas kernels  23.8 us (97%)
  between operations  0.64 us (3%)
    pallas_call x1, Pallas kernels, body(): pl.pallas_call(functools.partial(kernel, (groups, vocab, capacity)), out_...  23 us
    pallas_call x1, Pallas kernels, body(): pl.pallas_call(finish, out_shape=shapes, in_specs=[vmem] * 3, out_specs=(...  0.85 us

profile of v2, /device:TPU:0, one launch (start us, length us, event | category | flops | bytes accessed | tf_op | source)
XLA Modules:
  0.0 24.5 jit_solution(14627627082739710312)
XLA Ops:
  0.6 23.0 %shard_map.76 = (bf16[16,19008]{1,0:T(8,128)(2,1)S(1)}, f32[8,16]{1,0:T(8,128)S(1)}, f32[1,16]{1,0:T(1,128)S(1)}) custom-call(s32[8,8]{1,0:T(8,128)} %tok_hbm.1, s32[8]{0:T(128)} %lens_hbm.1, s32[8]{0:T(128)} %own_hbm.1, bf16[8,8,19008]{2,1,0:T(8,128)(2,1)} %x_hbm.1, bf16[8,8,19008]{2,1,0:T(8,128)(2,1)} %d_hbm.1), custom_call_target="tpu_custom_call" | custom-call | tf_op jit(solution)/shard_map/pallas_call | solution.py:435
  23.6 0.9 %shard_map.77 = (bf16[16,19008]{1,0:T(8,128)(2,1)}, f32[8,16]{1,0:T(8,128)}, f32[1,16]{1,0:T(1,128)}) custom-call(bf16[16,19008]{1,0:T(8,128)(2,1)S(1)} %get-tuple-element.9.block, f32[8,16]{1,0:T(8,128)S(1)} %get-tuple-element.10.accept, f32[1,16]{1,0:T(1,128)S(1)} %get-tuple-element.11.expected), custom_call_target="tpu_custom_call" | custom-call | tf_op jit(solution)/shard_map/pallas_call | solution.py:466

commit v3 on v2

--- a/solution.py
+++ b/solution.py
@@ -15,9 +15,9 @@
 TERMS = 3
 PARTS = 1
 PAIR = 2
-FIRST = 4
+FIRST = 2
 GROWTH = 3
-MOST = 40
+MOST = 24
 LOW = -1e30
 MESH = pl.DeviceIdType.MESH
 scope = jax.named_scope
@@ -297,8 +297,8 @@
     with scope("coef"):
         coef = weight / tree(jnp.add, [comm[norm_slot, p][0:1] for p in range(vocab)])
         coefs = [to_column(coef, n) for n in range(seqs)]
-        lowers = [to_column(coef * scale * mixing, n) for n in range(seqs)]
-        uppers = [to_column(coef * scale * (1.0 + mixing), n) for n in range(seqs)]
+        lowers = [coefs[n] * (scales[n] * mixing) for n in range(seqs)]
+        uppers = [coefs[n] * (scales[n] * (1.0 + mixing)) for n in range(seqs)]
 
     bounds = plan(tiles)
     chunks = len(bounds) - 1

time: 24.6 us -> 24.6 us (level)
  no operation moved by 1% of the time
where the time goes in v3:
time: 24.6 us; the launch traced here: 24.4 us
  Pallas kernels  23.8 us (97%)
  between operations  0.64 us (3%)
    pallas_call x1, Pallas kernels, body(): pl.pallas_call(functools.partial(kernel, (groups, vocab, capacity)), out_...  22.9 us
    pallas_call x1, Pallas kernels, body(): pl.pallas_call(finish, out_shape=shapes, in_specs=[vmem] * 3, out_specs=(...  0.85 us

profile of v3, /device:TPU:0, one launch (start us, length us, event | category | flops | bytes accessed | tf_op | source)
XLA Modules:
  0.0 24.4 jit_solution(2678510051681308194)
XLA Ops:
  0.6 22.9 %shard_map.76 = (bf16[16,19008]{1,0:T(8,128)(2,1)S(1)}, f32[8,16]{1,0:T(8,128)S(1)}, f32[1,16]{1,0:T(1,128)S(1)}) custom-call(s32[8,8]{1,0:T(8,128)} %tok_hbm.1, s32[8]{0:T(128)} %lens_hbm.1, s32[8]{0:T(128)} %own_hbm.1, bf16[8,8,19008]{2,1,0:T(8,128)(2,1)} %x_hbm.1, bf16[8,8,19008]{2,1,0:T(8,128)(2,1)} %d_hbm.1), custom_call_target="tpu_custom_call" | custom-call | tf_op jit(solution)/shard_map/pallas_call | solution.py:435
  23.6 0.9 %shard_map.77 = (bf16[16,19008]{1,0:T(8,128)(2,1)}, f32[8,16]{1,0:T(8,128)}, f32[1,16]{1,0:T(1,128)}) custom-call(bf16[16,19008]{1,0:T(8,128)(2,1)S(1)} %get-tuple-element.9.block, f32[8,16]{1,0:T(8,128)S(1)} %get-tuple-element.10.accept, f32[1,16]{1,0:T(1,128)S(1)} %get-tuple-element.11.expected), custom_call_target="tpu_custom_call" | custom-call | tf_op jit(solution)/shard_map/pallas_call | solution.py:466

commit v4 on v3

--- a/solution.py
+++ b/solution.py
@@ -33,6 +33,11 @@
         bounds.append(min(tiles, bounds[-1] + size))
         size = min(size * GROWTH, MOST)
     return bounds
+
+
+def landings(chunks):
+    cuts = sorted({0, max(0, chunks - 4), max(0, chunks - 2), max(0, chunks - 1), chunks})
+    return list(zip(cuts[:-1], cuts[1:]))
 
 
 def xor(value, mask):
@@ -308,8 +313,14 @@
         found = [(bounds[c] + a, size) for a, size in slabs(whole - bounds[c], PIECE)]
         return found + ([(full, 1)] if bounds[c + 1] > full else [])
 
-    def span(c):
-        return pl.ds(bounds[c] * LANES, (bounds[c + 1] - bounds[c]) * LANES)
+    groups_of = landings(chunks)
+
+    def landing(c):
+        return [first <= c < last for first, last in groups_of].index(True)
+
+    def span(c, last=None):
+        last = c + 1 if last is None else last
+        return pl.ds(bounds[c] * LANES, (bounds[last] - bounds[c]) * LANES)
 
     square = groups == 4
     near, far, across = xor(my_dp, 1), xor(my_dp, 2), xor(my_dp, 3)
@@ -317,7 +328,7 @@
     def ship(c, to):
         pltpu.make_async_remote_copy(
             src_ref=send.at[to, :, span(c)], dst_ref=landed.at[my_dp, :, span(c)],
-            send_sem=out_ssem, recv_sem=out_rsem.at[c],
+            send_sem=out_ssem, recv_sem=out_rsem.at[landing(c)],
             device_id=(to, my_v), device_id_type=MESH,
         ).start()
 
@@ -377,15 +388,15 @@
         accept_out[...] = final[:, :slots]
         expected_out[...] = final[0:1, half:half + slots]
 
-    for c in range(chunks):
+    for i, (c, last) in enumerate(groups_of):
         with scope(f"recv{c}"):
             pltpu.make_async_remote_copy(
-                src_ref=send.at[others, :, span(c)], dst_ref=landed.at[others, :, span(c)],
-                send_sem=out_ssem, recv_sem=out_rsem.at[c],
+                src_ref=send.at[others, :, span(c, last)], dst_ref=landed.at[others, :, span(c, last)],
+                send_sem=out_ssem, recv_sem=out_rsem.at[i],
                 device_id=(g_peers[0], my_v), device_id_type=MESH,
             ).wait_recv()
         with scope(f"gather{c}"):
-            for a, size in slabs(bounds[c + 1] - bounds[c], SLAB):
+            for a, size in slabs(bounds[last] - bounds[c], SLAB):
                 start = (bounds[c] + a) * LANES
                 columns = pl.ds(start, size * LANES)
                 pieces = [landed[g, :, columns].astype(jnp.float32) for g in range(groups)]
@@ -455,7 +466,7 @@
             dma(()),
             dma((BATCHES + 2,)),
             dma(()),
-            dma((chunks,)),
+            dma((len(landings(chunks)),)),
             dma(()),
             dma(()),
         ],

time: 24.6 us -> 24.5 us (level)
  no operation moved by 1% of the time
where the time goes in v4:
time: 24.5 us; the launch traced here: 24.4 us
  Pallas kernels  23.7 us (97%)
  between operations  0.64 us (3%)
    pallas_call x1, Pallas kernels, body(): pl.pallas_call(functools.partial(kernel, (groups, vocab, capacity)), out_...  22.9 us
    pallas_call x1, Pallas kernels, body(): pl.pallas_call(finish, out_shape=shapes, in_specs=[vmem] * 3, out_specs=(...  0.85 us

profile of v4, /device:TPU:0, one launch (start us, length us, event | category | flops | bytes accessed | tf_op | source)
XLA Modules:
  0.0 24.4 jit_solution(15789351380145689687)
XLA Ops:
  0.6 22.9 %shard_map.76 = (bf16[16,19008]{1,0:T(8,128)(2,1)S(1)}, f32[8,16]{1,0:T(8,128)S(1)}, f32[1,16]{1,0:T(1,128)S(1)}) custom-call(s32[8,8]{1,0:T(8,128)} %tok_hbm.1, s32[8]{0:T(128)} %lens_hbm.1, s32[8]{0:T(128)} %own_hbm.1, bf16[8,8,19008]{2,1,0:T(8,128)(2,1)} %x_hbm.1, bf16[8,8,19008]{2,1,0:T(8,128)(2,1)} %d_hbm.1), custom_call_target="tpu_custom_call" | custom-call | tf_op jit(solution)/shard_map/pallas_call | solution.py:446
  23.5 0.9 %shard_map.77 = (bf16[16,19008]{1,0:T(8,128)(2,1)}, f32[8,16]{1,0:T(8,128)}, f32[1,16]{1,0:T(1,128)}) custom-call(bf16[16,19008]{1,0:T(8,128)(2,1)S(1)} %get-tuple-element.9.block, f32[8,16]{1,0:T(8,128)S(1)} %get-tuple-element.10.accept, f32[1,16]{1,0:T(1,128)S(1)} %get-tuple-element.11.expected), custom_call_target="tpu_custom_call" | custom-call | tf_op jit(solution)/shard_map/pallas_call | solution.py:477
